TPU v7x, 256 devices: a whole 4x4x8 slice. The times are simulated.
256 devices in a mesh: dp: 8 (over x, core), fsdp: 8 (over z), mp: 4 (over y).
Axes of the slice: x: 4, y: 4, z: 8, core: 2. Of those that a mesh axis runs over, the one named last changes fastest.
Arguments:
- gradients: bfloat16 [64, 12, 2, 256, 1024], P(('dp', 'fsdp'), None, None, None, 'mp'), may hold values from -16 to 16
- master: float32 [12, 2, 256, 1024], P(None, None, ('dp', 'fsdp'), 'mp'), may hold values from -0.375 to 0.375
- teacher: float32 [12, 2, 256, 1024], P(None, None, ('dp', 'fsdp'), 'mp'), may hold values from -0.375 to 0.375
- first_moment: float32 [12, 2, 256, 1024], P(None, None, ('dp', 'fsdp'), 'mp'), may hold values from -2.2888184e-05 to 2.2888184e-05
- second_moment: float32 [12, 2, 256, 1024], P(None, None, ('dp', 'fsdp'), 'mp'), may hold values from 0 to 1, as said below
- layer_rates: float32 [12], replicated, may hold values from 0.02 to 0.2
Outputs:
- master_new: float32 [12, 2, 256, 1024], P(None, None, ('dp', 'fsdp'), 'mp')
- teacher_new: float32 [12, 2, 256, 1024], P(None, None, ('dp', 'fsdp'), 'mp')
- first_new: float32 [12, 2, 256, 1024], P(None, None, ('dp', 'fsdp'), 'mp')
- second_new: float32 [12, 2, 256, 1024], P(None, None, ('dp', 'fsdp'), 'mp')
- student_weights: bfloat16 [12, 2, 256, 1024], P(None, None, None, 'mp')
- teacher_weights: bfloat16 [12, 2, 256, 1024], P(None, None, None, 'mp')
Inputs may be any that keep to these rules, and one draw needn't show every extreme that they name: `second_moment`: every entry is positive.
All inputs are finite; a program needn't handle non-finite values.
Results may differ from a plain program's by a relative error of at most 0.0004.
Values may be sent and summed in bfloat16 or wider, within the bound.
No kernel may reach another device: no remote copies, remote signals or barrier semaphores. Data moves between devices by JAX's collectives and lax.ppermute only.
A program may use at most 64 MiB of HBM per device.

v0:
```python
import jax
import jax.numpy as jnp
from jax import lax
from jax.sharding import Mesh
from jax.sharding import PartitionSpec as P

DP = ("dp_0", "dp_1")
DP_FSDP_MP = ("dp_0", "dp_1", "fsdp", "mp")
DP_FSDP = ("dp_0", "dp_1", "fsdp")


CLIP_NORM = 0.1
BETA_ONE = 0.9
BETA_TWO = 0.999
BIAS_ONE = 1.0 - 0.9**50 * 0.9**50
BIAS_TWO = 1.0 - 0.999**50 * 0.999**50
ADAM_EPS = 1e-08
DECAY = 0.05
EMA_KEEP = 0.95


def cut_along(x, dim, length):
    before, after = (x.shape[:dim], x.shape[dim + 1 :])
    return jnp.moveaxis(x.reshape(*before, length, -1, *after), dim, 0)


def summed_on_arrival(x, axis, dim):
    length = lax.axis_size(axis)
    pieces = lax.all_to_all(cut_along(x, dim, length), axis, 0, 0, tiled=True)
    return jnp.sum(pieces, axis=0)


def by_axis(x, axes):
    for axis in axes:
        x = lax.psum(x, axis)
    return x


def side_by_side(arrays, axis, dim, along):
    ends, at = ([], 0)
    for a in arrays[:-1]:
        at += a.shape[along]
        ends.append(at)
    both = jnp.concatenate(arrays, axis=along)
    return tuple(jnp.split(lax.all_gather(both, axis, axis=dim, tiled=True), ends, axis=along))


def shards(gradients, master, teacher, first_moment, second_moment, layer_rates):
    own_grad = gradients[0].astype(jnp.float32)
    halfway = lax.psum_scatter(own_grad, DP, scatter_dimension=2, tiled=True)
    summed = summed_on_arrival(halfway, "fsdp", 2)
    mean_grad = summed / (lax.axis_size(DP) * lax.axis_size("fsdp"))
    norm_sq = by_axis(jnp.sum(mean_grad * mean_grad), DP_FSDP_MP)
    clip_factor = jnp.minimum(1.0, CLIP_NORM / (jnp.sqrt(norm_sq) + 1e-06))
    clipped = clip_factor * mean_grad
    first_new = BETA_ONE * first_moment + (1.0 - BETA_ONE) * clipped
    second_new = BETA_TWO * second_moment + (1.0 - BETA_TWO) * clipped * clipped
    direction = first_new / BIAS_ONE / (jnp.sqrt(second_new / BIAS_TWO) + ADAM_EPS) + DECAY * master
    layer_rate = layer_rates[:, None, None, None]
    master_new = master - layer_rate * direction
    teacher_new = EMA_KEEP * teacher + (1.0 - EMA_KEEP) * master_new
    student_half = master_new.astype(jnp.bfloat16)
    teacher_half = teacher_new.astype(jnp.bfloat16)
    partial_pair = side_by_side((student_half, teacher_half), "fsdp", 2, 0)
    student_weights, teacher_weights = side_by_side((partial_pair[0], partial_pair[1]), DP, 2, 0)
    return (master_new, teacher_new, first_new, second_new, student_weights, teacher_weights)


def solution(mesh):
    torus = Mesh(
        mesh.devices.reshape(4, 2, mesh.shape["fsdp"], mesh.shape["mp"]),
        ("dp_0", "dp_1", "fsdp", "mp"),
    )
    in_specs = (
        P(DP_FSDP, None, None, None, "mp"),
        P(None, None, DP_FSDP, "mp"),
        P(None, None, DP_FSDP, "mp"),
        P(None, None, DP_FSDP, "mp"),
        P(None, None, DP_FSDP, "mp"),
        P(),
    )
    out_specs = (
        P(None, None, DP_FSDP, "mp"),
        P(None, None, DP_FSDP, "mp"),
        P(None, None, DP_FSDP, "mp"),
        P(None, None, DP_FSDP, "mp"),
        P(None, None, None, "mp"),
        P(None, None, None, "mp"),
    )
    return jax.shard_map(
        shards, mesh=torus, in_specs=in_specs, out_specs=out_specs, check_vma=False
    )
```

profile of v0, /device:TPU:1, one launch (start us, length us, event | category | flops | bytes accessed | tf_op | source)
XLA Modules:
  0.0 220.4 jit_solution(2304604764215183388)
XLA Ops:
  7.2 0.0 reduce-scatter.2.cloned.1.call-start
  7.2 5.3 %bitcast_convert_fusion = f32[12,2,256,256]{3,2,1,0:T(8,128)} fusion(bf16[1,12,2,256,256]{4,3,2,1,0:T(8,128)(2,1)} %param.6), kind=kLoop, calls=%fused_computation | loop fusion | flops 1572864 | bytes 9437184 | tf_op jit(solution)/shard_map/convert_element_type | solution.py:49
  12.5 0.0 reduce-scatter.2.cloned.1.call-update
  12.6 0.0 copy-start.4
  12.6 0.0 all-gather.2.cloned.1.call-start
  12.7 48.3 %reduce-scatter.2.cloned.1.call-done = f32[12,2,32,256]{3,2,1,0:T(8,128)} async-done(((f32[12,2,256,256]{3,2,1,0:T(8,128)}), f32[12,2,32,256]{3,2,1,0:T(8,128)}) %reduce-scatter.2.cloned.1.call-update) | async-done | bytes 786448 | tf_op jit(solution)/shard_map/reduce_scatter | solution.py:50
  61.0 1.7 copy.36
  62.7 0.2 copy.37
  62.9 27.6 %all_to_all.5 = f32[8,12,2,4,256]{4,3,2,1,0:T(4,128)S(1)} all-to-all(f32[8,12,2,4,256]{4,3,2,1,0:T(4,128)S(1)} %copy.37), channel_id=1, replica_groups=mesh['dp_0'=4,'dp_1'=2,'fsdp'=8,'mp'=4] {'fsdp'}, dimensions={0} | all-to-all | bytes 1572864 | tf_op jit(solution)/shard_map/all_to_all | solution.py:29
  90.5 0.1 reduce_sum.18
  90.6 0.7 multiply_reduce_fusion
  91.3 11.4 %psum.28 = f32[]{:T(128)} all-reduce(f32[]{:T(128)} %multiply_reduce_fusion), channel_id=1, replica_groups=mesh['dp_0'=4,'dp_1'=2,'fsdp'=8,'mp'=4] {'dp_0'}, use_global_device_ids=true, to_apply=%region_3.0 | all-reduce | flops 1 | bytes 8 | tf_op jit(solution)/shard_map/psum | solution.py:35
  102.7 5.2 %psum.29 = f32[]{:T(128)} all-reduce(f32[]{:T(128)} %psum.28), channel_id=1, replica_groups=mesh['dp_0'=4,'dp_1'=2,'fsdp'=8,'mp'=4] {'dp_1'}, use_global_device_ids=true, to_apply=%region_4.0 | all-reduce | flops 1 | bytes 8 | tf_op jit(solution)/shard_map/psum | solution.py:35
  107.9 11.6 %psum.30 = f32[]{:T(128)} all-reduce(f32[]{:T(128)} %psum.29), channel_id=1, replica_groups=mesh['dp_0'=4,'dp_1'=2,'fsdp'=8,'mp'=4] {'fsdp'}, use_global_device_ids=true, to_apply=%region_5.0 | all-reduce | flops 1 | bytes 8 | tf_op jit(solution)/shard_map/psum | solution.py:35
  119.5 9.0 %psum.31 = f32[]{:T(128)} all-reduce(f32[]{:T(128)} %psum.30), channel_id=1, replica_groups=mesh['dp_0'=4,'dp_1'=2,'fsdp'=8,'mp'=4] {'mp'}, use_global_device_ids=true, to_apply=%region_6.0 | all-reduce | flops 1 | bytes 8 | tf_op jit(solution)/shard_map/psum | solution.py:35
  129.3 0.8 fusion.1
  130.1 0.7 fusion.3
  130.8 0.1 pad_maximum_fusion
  130.9 22.5 %all_gather.6 = bf16[24,2,32,256]{3,0,1,2:T(8,128)(2,1)} all-gather(bf16[24,2,4,256]{3,0,1,2:T(8,128)(2,1)S(1)} %copy.38), channel_id=1, replica_groups=mesh['dp_0'=4,'dp_1'=2,'fsdp'=8,'mp'=4] {'fsdp'}, dimensions={2}, use_global_device_ids=true | all-gather | bytes 884736 | tf_op jit(solution)/shard_map/all_gather | solution.py:45
  153.4 0.0 all-gather.2.cloned.1.call-update
  153.5 48.7 %all-gather.2.cloned.1.call-done = bf16[24,2,256,256]{3,0,1,2:T(8,128)(2,1)} async-done(((bf16[24,2,32,256]{3,0,1,2:T(8,128)(2,1)}), bf16[24,2,256,256]{3,0,1,2:T(8,128)(2,1)}) %all-gather.2.cloned.1.call-update) | async-done | bytes 6291472 | tf_op jit(solution)/shard_map/all_gather | solution.py:45
  202.2 4.5 %fusion.4 = (bf16[12,2,256,256]{3,0,1,2:T(8,128)(2,1)S(1)}, bf16[12,2,256,256]{3,0,1,2:T(8,128)(2,1)S(1)}) fusion(bf16[24,2,256,256]{3,0,1,2:T(8,128)(2,1)} %all-gather.2.cloned.1.call-done), kind=kLoop, calls=%fused_computation.10 | loop fusion | bytes 12582912 | tf_op jit(solution)/shard_map/split | solution.py:45
  206.7 3.5 %copy.40 = bf16[12,2,256,256]{3,2,1,0:T(8,128)(2,1)} copy(bf16[12,2,256,256]{3,0,1,2:T(8,128)(2,1)S(1)} %get-tuple-element.30) | data formatting | bytes 6291456
  210.1 3.5 %copy.39 = bf16[12,2,256,256]{3,2,1,0:T(8,128)(2,1)} copy(bf16[12,2,256,256]{3,0,1,2:T(8,128)(2,1)S(1)} %get-tuple-element.31) | data formatting | bytes 6291456
  (12 shorter events, 0.1 us)
Async XLA Ops:
  7.2 53.8 %reduce-scatter.2.cloned.1.call-start = ((), (), s32[]{:S(2)}) async-start(), calls=%async_computation.2 | async-start | bytes 7077888 | tf_op jit(solution)/shard_map/reduce_scatter | solution.py:50
  12.5 116.7 %copy-start.2 = (f32[12,2,4,256]{3,2,1,0:T(4,128)S(1)}, f32[12,2,4,256]{3,2,1,0:T(4,128)}, u32[]{:S(2)}) copy-start(f32[12,2,4,256]{3,2,1,0:T(4,128)} %param.7) | copy-start | bytes 294916
  12.6 116.7 %copy-start.3 = (f32[12,2,4,256]{3,2,1,0:T(4,128)S(1)}, f32[12,2,4,256]{3,2,1,0:T(4,128)}, u32[]{:S(2)}) copy-start(f32[12,2,4,256]{3,2,1,0:T(4,128)} %param.9) | copy-start | bytes 294916
  12.6 116.7 %copy-start.4 = (f32[12,2,4,256]{3,2,1,0:T(4,128)S(1)}, f32[12,2,4,256]{3,2,1,0:T(4,128)}, u32[]{:S(2)}) copy-start(f32[12,2,4,256]{3,2,1,0:T(4,128)} %param.10) | copy-start | bytes 294916
  12.6 116.7 %copy-start.5 = (f32[12]{0:T(128)S(1)}, f32[12]{0:T(128)}, u32[]{:S(2)}) copy-start(f32[12]{0:T(128)} %param.11) | copy-start | bytes 148
  12.6 117.5 %copy-start.1 = (f32[12,2,4,256]{3,2,1,0:T(4,128)S(1)}, f32[12,2,4,256]{3,2,1,0:T(4,128)}, u32[]{:S(2)}) copy-start(f32[12,2,4,256]{3,2,1,0:T(4,128)} %param.8) | copy-start | bytes 294916
  12.6 189.5 %all-gather.2.cloned.1.call-start = ((), (), s32[]{:S(2)}) async-start(), calls=%async_computation.3 | async-start | bytes 7077888 | tf_op jit(solution)/shard_map/all_gather | solution.py:45
  130.1 76.5 %copy-start = (f32[12,2,4,256]{3,2,1,0:T(4,128)}, f32[12,2,4,256]{3,2,1,0:T(4,128)S(1)}, u32[]{:S(2)}) copy-start(f32[12,2,4,256]{3,2,1,0:T(4,128)S(1)} %get-tuple-element.25) | copy-start | bytes 294916
Sparse Core Ops, SparseCore 0:
  12.7 48.2 reduce-scatter.1
  153.6 48.5 all-gather.1
where the time goes:
time: 221 us; the launch traced here: 220 us
  waiting for transfers between devices  97 us (44%)
  blocking collectives  87.3 us (40%)
  between operations  14.9 us (7%)
  local copies, waits for them, and re-layouts  13.4 us (6%)
  other arithmetic  7.69 us (3%)
    all_gather x1, waiting for transfers between devices, side_by_side(): lax.all_gather(both, axis, axis=dim, tiled=True)  48.7 us
    reduce_scatter x1, waiting for transfers between devices, shards(): halfway = lax.psum_scatter(own_grad, DP, scatter_dimension=2, tiled=True)  48.3 us
    psum x4, blocking collectives, by_axis(): x = lax.psum(x, axis)  37.2 us
    all_to_all x1, blocking collectives, summed_on_arrival(): pieces = lax.all_to_all(cut_along(x, dim, length), axis, 0, 0, tiled=True)  27.6 us
    all_gather x1, blocking collectives, side_by_side(): lax.all_gather(both, axis, axis=dim, tiled=True)  22.5 us
    unnamed x14, local copies, waits for them, and re-layouts  6.99 us
    convert_element_type x1, other arithmetic, shards(): own_grad = gradients[0].astype(jnp.float32)  5.31 us
    split x1, local copies, waits for them, and re-layouts, side_by_side(): jnp.split(lax.all_gather(both, axis, axis=dim, tiled=True), ends, axis=al...  4.48 us
  transfers between devices with their start and end apart: 2, of which 2 were waited for; matrix products, arithmetic and copies ran while one was open for 0% of the time, Pallas kernels for 0%

commit v1 on v0

v1 whole, which is shorter than its diff:
```python
import jax
import jax.numpy as jnp
from jax import lax
from jax.sharding import PartitionSpec as P

OWN = ("dp", "fsdp")
ALL = ("dp", "fsdp", "mp")

CLIP_NORM = 0.1
BETA_ONE = 0.9
BETA_TWO = 0.999
BIAS_ONE = 1.0 - 0.9**50 * 0.9**50
BIAS_TWO = 1.0 - 0.999**50 * 0.999**50
ADAM_EPS = 1e-08
DECAY = 0.05
EMA_KEEP = 0.95


def shards(gradients, master, teacher, first_moment, second_moment, layer_rates):
    own_grad = gradients[0].astype(jnp.float32)
    summed = lax.psum_scatter(own_grad, OWN, scatter_dimension=2, tiled=True)
    mean_grad = summed / 64.0
    norm_sq = lax.psum(jnp.sum(mean_grad * mean_grad), ALL)
    clip_factor = jnp.minimum(1.0, CLIP_NORM / (jnp.sqrt(norm_sq) + 1e-06))
    clipped = clip_factor * mean_grad
    first_new = BETA_ONE * first_moment + (1.0 - BETA_ONE) * clipped
    second_new = BETA_TWO * second_moment + (1.0 - BETA_TWO) * clipped * clipped
    direction = first_new / BIAS_ONE / (jnp.sqrt(second_new / BIAS_TWO) + ADAM_EPS) + DECAY * master
    layer_rate = layer_rates[:, None, None, None]
    master_new = master - layer_rate * direction
    teacher_new = EMA_KEEP * teacher + (1.0 - EMA_KEEP) * master_new
    student = lax.all_gather(master_new.astype(jnp.bfloat16), OWN, axis=2, tiled=True)
    teach = lax.all_gather(teacher_new.astype(jnp.bfloat16), OWN, axis=2, tiled=True)
    return (master_new, teacher_new, first_new, second_new, student, teach)


def solution(mesh):
    own = P(None, None, OWN, "mp")
    gathered = P(None, None, None, "mp")
    in_specs = (P(OWN, None, None, None, "mp"), own, own, own, own, P())
    out_specs = (own, own, own, own, gathered, gathered)
    return jax.shard_map(shards, mesh=mesh, in_specs=in_specs, out_specs=out_specs, check_vma=False)
```

time: 221 us -> 413 us (1.87)
  waiting for transfers between devices: 97 us -> 297 us
  blocking collectives: 87.3 us -> 78.7 us
    reduce_scatter x1, waiting for transfers between devices: 48.3 us -> 152 us  [shards(): summed = lax.psum_scatter(own_grad, OWN, scatter_dimension=2, tiled=True)]
    all_gather x1 -> x2, waiting for transfers between devices: 48.7 us -> 145 us  [the longest x1 73.9 us: shards(): lax.all_gather(teacher_new.astype(jnp.bfloat16), OWN, axis=2, tiled=True)]
    psum x4 -> x1, blocking collectives: 37.2 us -> 78.7 us  [shards(): norm_sq = lax.psum(jnp.sum(mean_grad * mean_grad), ALL)]
    all_to_all x1 -> x0, blocking collectives: 27.6 us -> none  [summed_on_arrival(): pieces = lax.all_to_all(cut_along(x, dim, length), axis, 0, 0, tiled=True)]
    all_gather x1 -> x0, blocking collectives: 22.5 us -> none  [side_by_side(): lax.all_gather(both, axis, axis=dim, tiled=True)]
    split x1 -> x0, local copies, waits for them, and re-layouts: 4.48 us -> none  [side_by_side(): jnp.split(lax.all_gather(both, axis, axis=dim, tiled=True), ends, axis=al...]
    unnamed x14 -> x16, local copies, waits for them, and re-layouts: 6.99 us -> 11.4 us
  transfers between devices with their start and end apart: 2 -> 3, of which waited for: 2 -> 3; matrix products, arithmetic and copies ran while one was open for 0% -> 2% of each run, Pallas kernels for 0% -> 0%
where the time goes in v1:
time: 413 us
  waiting for transfers between devices  297 us (72%)
  blocking collectives  78.7 us (19%)
  between operations  14.5 us (4%)
  local copies, waits for them, and re-layouts  12.7 us (3%)
  other arithmetic  9.68 us (2%)
    reduce_scatter x1, waiting for transfers between devices, shards(): summed = lax.psum_scatter(own_grad, OWN, scatter_dimension=2, tiled=True)  152 us
    psum x1, blocking collectives, shards(): norm_sq = lax.psum(jnp.sum(mean_grad * mean_grad), ALL)  78.7 us
    all_gather x1, waiting for transfers between devices, shards(): lax.all_gather(teacher_new.astype(jnp.bfloat16), OWN, axis=2, tiled=True)  73.9 us
    all_gather x1, waiting for transfers between devices, shards(): lax.all_gather(master_new.astype(jnp.bfloat16), OWN, axis=2, tiled=True)  71.5 us
    unnamed x16, local copies, waits for them, and re-layouts  11.4 us
  transfers between devices with their start and end apart: 3, of which 3 were waited for; matrix products, arithmetic and copies ran while one was open for 2% of the time, Pallas kernels for 0%

profile of v1, /device:TPU:1, one launch (start us, length us, event | category | flops | bytes accessed | tf_op | source)
XLA Modules:
  0.0 413.0 jit_solution(480780248336302537)
XLA Ops:
  7.2 0.0 reduce-scatter.2.cloned.1.call-start
  7.2 7.0 %bitcast_convert_fusion = f32[12,2,256,256]{3,0,1,2:T(8,128)} fusion(bf16[1,12,2,256,256]{4,3,2,1,0:T(8,128)(2,1)} %param.6), kind=kLoop, calls=%fused_computation | loop fusion | flops 1572864 | bytes 9437184 | tf_op jit(solution)/shard_map/convert_element_type | solution.py:20
  14.2 0.0 copy-start.4
  14.2 0.0 reduce-scatter.2.cloned.1.call-update
  14.3 0.0 all-gather.3.cloned.1.call-start
  14.3 151.8 %reduce-scatter.2.cloned.1.call-done = f32[12,2,4,256]{3,0,1,2:T(8,128)} async-done(((f32[12,2,256,256]{3,0,1,2:T(8,128)}), f32[12,2,4,256]{3,0,1,2:T(8,128)}) %reduce-scatter.2.cloned.1.call-update) | async-done | bytes 98320 | tf_op jit(solution)/shard_map/reduce_scatter | solution.py:21
  166.1 1.5 multiply_reduce_fusion
  167.6 78.7 %psum.7 = f32[]{:T(128)} all-reduce(f32[]{:T(128)} %multiply_reduce_fusion), channel_id=1, replica_groups=mesh['dp'=8,'fsdp'=8,'mp'=4] {'dp','fsdp','mp'}, use_global_device_ids=true, to_apply=%region_2.0 | all-reduce | flops 1 | bytes 8 | tf_op jit(solution)/shard_map/psum | solution.py:23
  247.1 0.0 copy-done
  247.1 0.0 copy-done.1
  247.1 1.1 fusion.5
  248.3 0.7 copy.18
  248.9 0.0 all-gather.3.cloned.1.call-update
  249.0 0.0 all-gather.5.cloned.1.call-start
  249.0 0.7 copy.19
  249.7 0.0 all-gather.5.cloned.1.call-update
  249.7 0.7 copy.20
  250.4 0.7 copy.21
  251.1 0.7 copy.22
  251.8 0.7 copy.23
  252.5 71.5 %all-gather.3.cloned.1.call-done = bf16[12,2,256,256]{3,1,0,2:T(2,128)(2,1)} async-done(((bf16[12,2,4,256]{3,1,0,2:T(2,128)(2,1)}), bf16[12,2,256,256]{3,1,0,2:T(2,128)(2,1)}) %all-gather.3.cloned.1.call-update) | async-done | bytes 3145744 | tf_op jit(solution)/shard_map/all_gather | solution.py:32
  324.1 4.3 %copy.24 = bf16[12,2,256,256]{3,2,1,0:T(8,128)(2,1)} copy(bf16[12,2,256,256]{3,1,0,2:T(2,128)(2,1)} %all-gather.3.cloned.1.call-done) | data formatting | bytes 6291456
  328.4 73.9 %all-gather.5.cloned.1.call-done = bf16[12,2,256,256]{3,1,0,2:T(2,128)(2,1)} async-done(((bf16[12,2,4,256]{3,1,0,2:T(2,128)(2,1)}), bf16[12,2,256,256]{3,1,0,2:T(2,128)(2,1)}) %all-gather.5.cloned.1.call-update) | async-done | bytes 3145744 | tf_op jit(solution)/shard_map/all_gather | solution.py:33
  402.2 4.3 %copy.25 = bf16[12,2,256,256]{3,2,1,0:T(8,128)(2,1)} copy(bf16[12,2,256,256]{3,1,0,2:T(2,128)(2,1)} %all-gather.5.cloned.1.call-done) | data formatting | bytes 6291456
  (8 shorter events, 0.0 us)
Async XLA Ops:
  7.2 158.9 %reduce-scatter.2.cloned.1.call-start = ((), (), s32[]{:S(2)}) async-start(), calls=%async_computation.1 | async-start | bytes 8519680 | tf_op jit(solution)/shard_map/reduce_scatter | solution.py:21
  14.2 232.9 %copy-start = (f32[12,2,4,256]{3,2,1,0:T(4,128)S(1)}, f32[12,2,4,256]{3,2,1,0:T(4,128)}, u32[]{:S(2)}) copy-start(f32[12,2,4,256]{3,2,1,0:T(4,128)} %param.8) | copy-start | bytes 294916
  14.2 232.9 %copy-start.1 = (f32[12,2,4,256]{3,2,1,0:T(4,128)S(1)}, f32[12,2,4,256]{3,2,1,0:T(4,128)}, u32[]{:S(2)}) copy-start(f32[12,2,4,256]{3,2,1,0:T(4,128)} %param.7) | copy-start | bytes 294916
  14.2 232.9 %copy-start.2 = (f32[12,2,4,256]{3,2,1,0:T(4,128)S(1)}, f32[12,2,4,256]{3,2,1,0:T(4,128)}, u32[]{:S(2)}) copy-start(f32[12,2,4,256]{3,2,1,0:T(4,128)} %param.9) | copy-start | bytes 294916
  14.2 232.9 %copy-start.3 = (f32[12,2,4,256]{3,2,1,0:T(4,128)S(1)}, f32[12,2,4,256]{3,2,1,0:T(4,128)}, u32[]{:S(2)}) copy-start(f32[12,2,4,256]{3,2,1,0:T(4,128)} %param.10) | copy-start | bytes 294916
  14.2 232.9 %copy-start.4 = (f32[12]{0:T(128)S(1)}, f32[12]{0:T(128)}, u32[]{:S(2)}) copy-start(f32[12]{0:T(128)} %param.11) | copy-start | bytes 148
  14.3 309.8 %all-gather.3.cloned.1.call-start = ((), (), s32[]{:S(2)}) async-start(), calls=%async_computation.2 | async-start | bytes 3194880 | tf_op jit(solution)/shard_map/all_gather | solution.py:32
  249.0 153.3 %all-gather.5.cloned.1.call-start = ((), (), s32[]{:S(2)}) async-start(), calls=%async_computation.3 | async-start | bytes 3194880 | tf_op jit(solution)/shard_map/all_gather | solution.py:33
Sparse Core Ops, SparseCore 0:
  14.4 151.6 reduce-scatter.1
  249.1 74.9 all-gather.2
  326.8 75.3 all-gather.4
